TPU v7x, 32 devices: a whole 2x2x4 slice. The times are simulated.
32 devices in a mesh: seq: 8 (over y, x, core), tensor: 4 (over z).
Axes of the slice: x: 2, y: 2, z: 4, core: 2. Of those that a mesh axis runs over, the one named last changes fastest.
Arguments:
- tokens: bfloat16 [5760, 1536], P('seq'), may hold values from -6 to 6
- norm_gain: float32 [1536], replicated, may hold values from 0.1 to 1.9
- w_qkv: bfloat16 [1536, 3, 1536], P(None, None, 'tensor'), may hold values from -8 to 8
- w_out: bfloat16 [1536, 1536], P('tensor'), may hold values from -0.15625 to 0.15625
- post_gain: float32 [1536], replicated, may hold values from 0.1 to 1.9
- w_up: bfloat16 [1536, 6144], P(None, 'tensor'), may hold values from -0.15625 to 0.15625
- w_down: bfloat16 [6144, 1536], P('tensor'), may hold values from -0.078125 to 0.078125
Outputs:
- layer_out: bfloat16 [5760, 1536], P('seq')
All inputs are finite; a program needn't handle non-finite values.
Results may differ from a plain program's by a relative error of at most 0.015.
Values may be sent and summed in bfloat16 or wider, within the bound.
A program may use at most 128 MiB of HBM per device.

v0:
```python
import jax
import jax.numpy as jnp
from jax import lax
from jax.sharding import PartitionSpec as P

HD = 48


def layer_norm(values, gain):
    mean = jnp.mean(values, axis=-1, keepdims=True)
    centred = values - mean
    var = jnp.mean(centred * centred, axis=-1, keepdims=True)
    return centred * lax.rsqrt(var + 1e-05) * gain


def attend_block(carry, queries, key_rows, value_rows, scale):
    peak, total, accum = carry
    heads = queries.shape[1]
    keys = key_rows.reshape(key_rows.shape[0], heads, -1)
    values = value_rows.reshape(value_rows.shape[0], heads, -1)
    scores = jnp.einsum("qhd,khd->hqk", queries, keys, preferred_element_type=jnp.float32) * scale
    fresh = jnp.maximum(peak, jnp.max(scores, axis=-1))
    factor = jnp.exp(peak - fresh)
    weights = jnp.exp(scores - fresh[..., None])
    total = total * factor + jnp.sum(weights, axis=-1)
    accum = accum * factor[..., None] + jnp.einsum(
        "hqk,khd->hqd", weights.astype(jnp.bfloat16), values, preferred_element_type=jnp.float32
    )
    return (fresh, total, accum)


def empty_state(rows, heads, width):
    return (
        jnp.full((heads, rows), -1e30, jnp.float32),
        jnp.zeros((heads, rows), jnp.float32),
        jnp.zeros((heads, rows, width), jnp.float32),
    )


def per_device(tokens, norm_gain, w_qkv, w_out, post_gain, w_up, w_down):
    rows = tokens.shape[0]
    local_heads = w_qkv.shape[2] // HD
    scale = 1.0 / HD**0.5
    base = tokens.astype(jnp.float32)
    normed = layer_norm(base, norm_gain).astype(jnp.bfloat16)
    qkv = jnp.dot(
        normed, w_qkv.reshape(w_qkv.shape[0], -1), preferred_element_type=jnp.float32
    ).astype(jnp.bfloat16)
    span = local_heads * HD
    query = qkv[:, :span]
    key = qkv[:, span : 2 * span]
    value = qkv[:, 2 * span :]
    query3 = query.reshape(rows, local_heads, HD)
    key_piece = lax.all_gather(key, "seq", axis=0, tiled=True)
    value_piece = lax.all_gather(value, "seq", axis=0, tiled=True)
    count = key_piece.shape[0]
    block = count
    while block > 1024 and block % 2 == 0:
        block = block // 2

    def step(index, state):
        first = index * block
        key_block = lax.dynamic_slice_in_dim(key_piece, first, block, 0)
        value_block = lax.dynamic_slice_in_dim(value_piece, first, block, 0)
        return attend_block(state, query3, key_block, value_block, scale)

    peak, total, accum = lax.fori_loop(0, count // block, step, empty_state(rows, local_heads, HD))
    result = accum / total[..., None]
    attended = jnp.transpose(result, (1, 0, 2)).reshape(rows, span).astype(jnp.bfloat16)
    attn_term = jnp.dot(attended, w_out, preferred_element_type=jnp.float32)
    mixed = base + lax.psum(attn_term.astype(jnp.bfloat16), "tensor").astype(jnp.float32)
    post = layer_norm(mixed, post_gain).astype(jnp.bfloat16)
    hidden = jax.nn.gelu(
        jnp.dot(post, w_up, preferred_element_type=jnp.float32), approximate=True
    ).astype(jnp.bfloat16)
    mlp_term = jnp.dot(hidden, w_down, preferred_element_type=jnp.float32)
    return (mixed + lax.psum(mlp_term.astype(jnp.bfloat16), "tensor").astype(jnp.float32)).astype(
        jnp.bfloat16
    )


def solution(mesh):
    placed = (
        P("seq", None),
        P(),
        P(None, None, "tensor"),
        P("tensor", None),
        P(),
        P(None, "tensor"),
        P("tensor", None),
    )
    return jax.shard_map(
        per_device, mesh=mesh, in_specs=placed, out_specs=P("seq", None), check_vma=False
    )
```

profile of v0, /device:TPU:0, one launch (start us, length us, event | category | flops | bytes accessed | tf_op | source)
XLA Modules:
  0.0 578.7 jit_solution(9343756593150286933)
XLA Ops:
  24.9 39.2 %all-gather.5.cloned.1.call-done = bf16[5760,384]{1,0:T(8,128)(2,1)} async-done(((bf16[720,384]{1,0:T(8,128)(2,1)}), bf16[5760,384]{1,0:T(8,128)(2,1)}) %all-gather.5.cloned.1.call-update) | async-done | bytes 4423696 | tf_op jit(solution)/shard_map/all_gather | solution.py:55
  64.0 39.5 %all-gather.3.cloned.1.call-done = bf16[5760,384]{1,0:T(8,128)(2,1)} async-done(((bf16[720,384]{1,0:T(8,128)(2,1)}), bf16[5760,384]{1,0:T(8,128)(2,1)}) %all-gather.3.cloned.1.call-update) | async-done | bytes 4423696 | tf_op jit(solution)/shard_map/all_gather | solution.py:54
  103.5 264.1 %while.18 = (s32[]{:T(128)}, f32[8,720]{1,0:T(8,128)}, f32[8,720]{1,0:T(8,128)}, f32[8,720,48]{1,2,0:T(8,128)}, bf16[5760,384]{1,0:T(8,128)(2,1)}, /*index=5*/bf...) while((s32[]{:T(128)}, f32[8,720]{1,0:T(8,128)}, ...), condition=%wide.region_5.0_spmd.clone, body=%wide.region_2.0_spmd.clone.sunk | while | flops 830298240 | bytes 67369216 | solution.py:67
  114.5 9.7 %fusion.56 = f32[8,720]{1,0:T(8,128)} fusion(f32[8,720,720]{2,1,0:T(8,128)} %get-tuple-element.244, f32[8,720]{1,0:T(8,128)} %select_maximum_fusion.2), kind=kLoop, calls=%fused_computation.4.clone.1 | loop fusion | flops 12435840 | bytes 16634880 | tf_op jit(solution)/shard_map/while/body/eval_jaxpr/reduce_sum | solution.py:25
  125.6 9.2 %fusion.58 = f32[8,720,48]{1,2,0:T(8,128)S(1)} fusion(bf16[720,8,48]{0,2,1:T(8,128)(2,1)S(1)} %bitcast.43, f32[8,720,720]{2,1,0:T(8,128)} %get-tuple-element.244, f32[8,720]{1,0:T(8,128)} %select_maximum_fusion.2, f32[8,720,48]{1,2,0:T(8,128)S(1)} %copy-done.3, f32[8,720]{1,0:T(8,128)S(1)} %get-tuple-element.247, pred[]{:T(512)S(6)} %compare.3), kind=kOutput, calls=%fused_computation.6.clone.1 | convolution fusion | flops 411402240 | bytes 19399680 | tf_op jit(solution)/shard_map/while/body/eval_jaxpr/hqk,khd->hqd/dot_general | solution.py:26
  147.6 9.7 %fusion.56 = f32[8,720]{1,0:T(8,128)} fusion(f32[8,720,720]{2,1,0:T(8,128)} %get-tuple-element.244, f32[8,720]{1,0:T(8,128)} %select_maximum_fusion.2), kind=kLoop, calls=%fused_computation.4.clone.1 | loop fusion | flops 12435840 | bytes 16634880 | tf_op jit(solution)/shard_map/while/body/eval_jaxpr/reduce_sum | solution.py:25
  158.7 9.2 %fusion.58 = f32[8,720,48]{1,2,0:T(8,128)S(1)} fusion(bf16[720,8,48]{0,2,1:T(8,128)(2,1)S(1)} %bitcast.43, f32[8,720,720]{2,1,0:T(8,128)} %get-tuple-element.244, f32[8,720]{1,0:T(8,128)} %select_maximum_fusion.2, f32[8,720,48]{1,2,0:T(8,128)S(1)} %copy-done.3, f32[8,720]{1,0:T(8,128)S(1)} %get-tuple-element.247, pred[]{:T(512)S(6)} %compare.3), kind=kOutput, calls=%fused_computation.6.clone.1 | convolution fusion | flops 411402240 | bytes 19399680 | tf_op jit(solution)/shard_map/while/body/eval_jaxpr/hqk,khd->hqd/dot_general | solution.py:26
  180.7 9.7 %fusion.56 = f32[8,720]{1,0:T(8,128)} fusion(f32[8,720,720]{2,1,0:T(8,128)} %get-tuple-element.244, f32[8,720]{1,0:T(8,128)} %select_maximum_fusion.2), kind=kLoop, calls=%fused_computation.4.clone.1 | loop fusion | flops 12435840 | bytes 16634880 | tf_op jit(solution)/shard_map/while/body/eval_jaxpr/reduce_sum | solution.py:25
  191.9 9.2 %fusion.58 = f32[8,720,48]{1,2,0:T(8,128)S(1)} fusion(bf16[720,8,48]{0,2,1:T(8,128)(2,1)S(1)} %bitcast.43, f32[8,720,720]{2,1,0:T(8,128)} %get-tuple-element.244, f32[8,720]{1,0:T(8,128)} %select_maximum_fusion.2, f32[8,720,48]{1,2,0:T(8,128)S(1)} %copy-done.3, f32[8,720]{1,0:T(8,128)S(1)} %get-tuple-element.247, pred[]{:T(512)S(6)} %compare.3), kind=kOutput, calls=%fused_computation.6.clone.1 | convolution fusion | flops 411402240 | bytes 19399680 | tf_op jit(solution)/shard_map/while/body/eval_jaxpr/hqk,khd->hqd/dot_general | solution.py:26
  213.8 9.7 %fusion.56 = f32[8,720]{1,0:T(8,128)} fusion(f32[8,720,720]{2,1,0:T(8,128)} %get-tuple-element.244, f32[8,720]{1,0:T(8,128)} %select_maximum_fusion.2), kind=kLoop, calls=%fused_computation.4.clone.1 | loop fusion | flops 12435840 | bytes 16634880 | tf_op jit(solution)/shard_map/while/body/eval_jaxpr/reduce_sum | solution.py:25
  225.0 9.2 %fusion.58 = f32[8,720,48]{1,2,0:T(8,128)S(1)} fusion(bf16[720,8,48]{0,2,1:T(8,128)(2,1)S(1)} %bitcast.43, f32[8,720,720]{2,1,0:T(8,128)} %get-tuple-element.244, f32[8,720]{1,0:T(8,128)} %select_maximum_fusion.2, f32[8,720,48]{1,2,0:T(8,128)S(1)} %copy-done.3, f32[8,720]{1,0:T(8,128)S(1)} %get-tuple-element.247, pred[]{:T(512)S(6)} %compare.3), kind=kOutput, calls=%fused_computation.6.clone.1 | convolution fusion | flops 411402240 | bytes 19399680 | tf_op jit(solution)/shard_map/while/body/eval_jaxpr/hqk,khd->hqd/dot_general | solution.py:26
  246.9 9.7 %fusion.56 = f32[8,720]{1,0:T(8,128)} fusion(f32[8,720,720]{2,1,0:T(8,128)} %get-tuple-element.244, f32[8,720]{1,0:T(8,128)} %select_maximum_fusion.2), kind=kLoop, calls=%fused_computation.4.clone.1 | loop fusion | flops 12435840 | bytes 16634880 | tf_op jit(solution)/shard_map/while/body/eval_jaxpr/reduce_sum | solution.py:25
  258.1 9.2 %fusion.58 = f32[8,720,48]{1,2,0:T(8,128)S(1)} fusion(bf16[720,8,48]{0,2,1:T(8,128)(2,1)S(1)} %bitcast.43, f32[8,720,720]{2,1,0:T(8,128)} %get-tuple-element.244, f32[8,720]{1,0:T(8,128)} %select_maximum_fusion.2, f32[8,720,48]{1,2,0:T(8,128)S(1)} %copy-done.3, f32[8,720]{1,0:T(8,128)S(1)} %get-tuple-element.247, pred[]{:T(512)S(6)} %compare.3), kind=kOutput, calls=%fused_computation.6.clone.1 | convolution fusion | flops 411402240 | bytes 19399680 | tf_op jit(solution)/shard_map/while/body/eval_jaxpr/hqk,khd->hqd/dot_general | solution.py:26
  270.1 8.6 %bitcast_reduce_fusion.2 = (f32[8,720]{1,0:T(8,128)S(1)}, f32[8,720,720]{2,1,0:T(8,128)}) fusion(bf16[720,8,48]{0,2,1:T(8,128)(2,1)S(1)} %bitcast.44, bf16[720,8,48]{0,2,1:T(8,128)(2,1)S(1)} %get-tuple-element.275), kind=kOutput, calls=%fused_computation.1.clone.1 | convolution fusion | flops 406419840 | bytes 17717760 | tf_op jit(solution)/shard_map/while/body/eval_jaxpr/qhd,khd->hqk/dot_general | solution.py:21
  280.0 9.7 %fusion.56 = f32[8,720]{1,0:T(8,128)} fusion(f32[8,720,720]{2,1,0:T(8,128)} %get-tuple-element.244, f32[8,720]{1,0:T(8,128)} %select_maximum_fusion.2), kind=kLoop, calls=%fused_computation.4.clone.1 | loop fusion | flops 12435840 | bytes 16634880 | tf_op jit(solution)/shard_map/while/body/eval_jaxpr/reduce_sum | solution.py:25
  291.2 9.2 %fusion.58 = f32[8,720,48]{1,2,0:T(8,128)S(1)} fusion(bf16[720,8,48]{0,2,1:T(8,128)(2,1)S(1)} %bitcast.43, f32[8,720,720]{2,1,0:T(8,128)} %get-tuple-element.244, f32[8,720]{1,0:T(8,128)} %select_maximum_fusion.2, f32[8,720,48]{1,2,0:T(8,128)S(1)} %copy-done.3, f32[8,720]{1,0:T(8,128)S(1)} %get-tuple-element.247, pred[]{:T(512)S(6)} %compare.3), kind=kOutput, calls=%fused_computation.6.clone.1 | convolution fusion | flops 411402240 | bytes 19399680 | tf_op jit(solution)/shard_map/while/body/eval_jaxpr/hqk,khd->hqd/dot_general | solution.py:26
  303.2 8.6 %bitcast_reduce_fusion.2 = (f32[8,720]{1,0:T(8,128)S(1)}, f32[8,720,720]{2,1,0:T(8,128)}) fusion(bf16[720,8,48]{0,2,1:T(8,128)(2,1)S(1)} %bitcast.44, bf16[720,8,48]{0,2,1:T(8,128)(2,1)S(1)} %get-tuple-element.275), kind=kOutput, calls=%fused_computation.1.clone.1 | convolution fusion | flops 406419840 | bytes 17717760 | tf_op jit(solution)/shard_map/while/body/eval_jaxpr/qhd,khd->hqk/dot_general | solution.py:21
  313.1 9.7 %fusion.56 = f32[8,720]{1,0:T(8,128)} fusion(f32[8,720,720]{2,1,0:T(8,128)} %get-tuple-element.244, f32[8,720]{1,0:T(8,128)} %select_maximum_fusion.2), kind=kLoop, calls=%fused_computation.4.clone.1 | loop fusion | flops 12435840 | bytes 16634880 | tf_op jit(solution)/shard_map/while/body/eval_jaxpr/reduce_sum | solution.py:25
  324.3 9.2 %fusion.58 = f32[8,720,48]{1,2,0:T(8,128)S(1)} fusion(bf16[720,8,48]{0,2,1:T(8,128)(2,1)S(1)} %bitcast.43, f32[8,720,720]{2,1,0:T(8,128)} %get-tuple-element.244, f32[8,720]{1,0:T(8,128)} %select_maximum_fusion.2, f32[8,720,48]{1,2,0:T(8,128)S(1)} %copy-done.3, f32[8,720]{1,0:T(8,128)S(1)} %get-tuple-element.247, pred[]{:T(512)S(6)} %compare.3), kind=kOutput, calls=%fused_computation.6.clone.1 | convolution fusion | flops 411402240 | bytes 19399680 | tf_op jit(solution)/shard_map/while/body/eval_jaxpr/hqk,khd->hqd/dot_general | solution.py:26
  346.2 9.7 %fusion.56 = f32[8,720]{1,0:T(8,128)} fusion(f32[8,720,720]{2,1,0:T(8,128)} %get-tuple-element.244, f32[8,720]{1,0:T(8,128)} %select_maximum_fusion.2), kind=kLoop, calls=%fused_computation.4.clone.1 | loop fusion | flops 12435840 | bytes 16634880 | tf_op jit(solution)/shard_map/while/body/eval_jaxpr/reduce_sum | solution.py:25
  357.4 9.2 %fusion.58 = f32[8,720,48]{1,2,0:T(8,128)S(1)} fusion(bf16[720,8,48]{0,2,1:T(8,128)(2,1)S(1)} %bitcast.43, f32[8,720,720]{2,1,0:T(8,128)} %get-tuple-element.244, f32[8,720]{1,0:T(8,128)} %select_maximum_fusion.2, f32[8,720,48]{1,2,0:T(8,128)S(1)} %copy-done.3, f32[8,720]{1,0:T(8,128)S(1)} %get-tuple-element.247, pred[]{:T(512)S(6)} %compare.3), kind=kOutput, calls=%fused_computation.6.clone.1 | convolution fusion | flops 411402240 | bytes 19399680 | tf_op jit(solution)/shard_map/while/body/eval_jaxpr/hqk,khd->hqd/dot_general | solution.py:26
  372.0 90.0 %all-reduce.3.cloned.1.call-done = bf16[720,1536]{1,0:T(8,128)(2,1)} async-done(((bf16[720,1536]{1,0:T(8,128)(2,1)}), bf16[720,1536]{1,0:T(8,128)(2,1)}) %all-reduce.3.cloned.1.call-update) | async-done | bytes 2211856 | tf_op jit(solution)/shard_map/psum | solution.py:71
  465.4 12.9 %convolution_convert_fusion = bf16[720,1536]{1,0:T(8,128)(2,1)} fusion(bf16[1536,1536]{1,0:T(8,128)(2,1)} %param.15, bf16[1536,1536]{1,0:T(8,128)(2,1)} %param.14, bf16[720,1536]{1,0:T(8,128)(2,1)} %all-reduce.3.cloned.1.call-done, bf16[720,1536]{1,0:T(8,128)(2,1)S(1)} %copy-done.2, f32[1536]{0:T(1024)S(1)} %copy-done.8, f32[720]{0:T(1024)S(1)} %add_rsqrt_fusion, ...), kind=kOutput, calls=%fused_computation.36 | convolution fusion | flops 6813573120 | bytes 16084608 | tf_op jit(solution)/shard_map/dot_general | solution.py:76
  478.4 89.3 %all-reduce.5.cloned.1.call-done = bf16[720,1536]{1,0:T(8,128)(2,1)} async-done(((bf16[720,1536]{1,0:T(8,128)(2,1)}), bf16[720,1536]{1,0:T(8,128)(2,1)}) %all-reduce.5.cloned.1.call-update) | async-done | bytes 2211856 | tf_op jit(solution)/shard_map/psum | solution.py:77
  (140 shorter events, 126.0 us)
Async XLA Ops:
  6.5 362.4 %copy-start = (bf16[384,1536]{1,0:T(8,128)(2,1)S(1)}, bf16[384,1536]{1,0:T(8,128)(2,1)}, u32[]{:S(2)}) copy-start(bf16[384,1536]{1,0:T(8,128)(2,1)} %param.12) | copy-start | bytes 3538948
  6.5 57.5 %all-gather.5.cloned.1.call-start = ((), (), s32[]{:S(2)}) async-start(), calls=%async_computation.1 | async-start | bytes 4976640 | tf_op jit(solution)/shard_map/all_gather | solution.py:55
  8.6 8.6 %copy-start.1 = (bf16[720,1536]{1,0:T(8,128)(2,1)S(1)}, bf16[720,1536]{1,0:T(8,128)(2,1)}, u32[]{:S(2)}) copy-start(bf16[720,1536]{1,0:T(8,128)(2,1)} %param.9) | copy-start | bytes 6635524
  23.6 79.9 %all-gather.3.cloned.1.call-start = ((), (), s32[]{:S(2)}) async-start(), calls=%async_computation | async-start | bytes 4976640 | tf_op jit(solution)/shard_map/all_gather | solution.py:54
  24.3 437.7 %all-reduce.3.cloned.1.call-start = ((), (), s32[]{:S(2)}) async-start(), calls=%async_computation.2 | async-start | bytes 4423680 | tf_op jit(solution)/shard_map/psum | solution.py:71
  114.5 11.1 %copy-start.3 = (f32[8,720,48]{1,2,0:T(8,128)S(1)}, f32[8,720,48]{1,2,0:T(8,128)}, u32[]{:S(2)}) copy-start(f32[8,720,48]{1,2,0:T(8,128)} %get-tuple-element.262) | copy-start | bytes 3317764 | tf_op jit(solution)/shard_map/while
  125.6 9.2 %copy-start.6 = (f32[8,720]{1,0:T(8,128)S(1)}, f32[8,720]{1,0:T(8,128)}, u32[]{:S(2)}) copy-start(f32[8,720]{1,0:T(8,128)} %select_maximum_fusion.2) | copy-start | bytes 69124 | tf_op jit(solution)/shard_map/while
  147.6 11.2 %copy-start.3 = (f32[8,720,48]{1,2,0:T(8,128)S(1)}, f32[8,720,48]{1,2,0:T(8,128)}, u32[]{:S(2)}) copy-start(f32[8,720,48]{1,2,0:T(8,128)} %get-tuple-element.262) | copy-start | bytes 3317764 | tf_op jit(solution)/shard_map/while
  158.7 9.2 %copy-start.6 = (f32[8,720]{1,0:T(8,128)S(1)}, f32[8,720]{1,0:T(8,128)}, u32[]{:S(2)}) copy-start(f32[8,720]{1,0:T(8,128)} %select_maximum_fusion.2) | copy-start | bytes 69124 | tf_op jit(solution)/shard_map/while
  180.7 11.2 %copy-start.3 = (f32[8,720,48]{1,2,0:T(8,128)S(1)}, f32[8,720,48]{1,2,0:T(8,128)}, u32[]{:S(2)}) copy-start(f32[8,720,48]{1,2,0:T(8,128)} %get-tuple-element.262) | copy-start | bytes 3317764 | tf_op jit(solution)/shard_map/while
  191.8 9.2 %copy-start.6 = (f32[8,720]{1,0:T(8,128)S(1)}, f32[8,720]{1,0:T(8,128)}, u32[]{:S(2)}) copy-start(f32[8,720]{1,0:T(8,128)} %select_maximum_fusion.2) | copy-start | bytes 69124 | tf_op jit(solution)/shard_map/while
  213.8 11.2 %copy-start.3 = (f32[8,720,48]{1,2,0:T(8,128)S(1)}, f32[8,720,48]{1,2,0:T(8,128)}, u32[]{:S(2)}) copy-start(f32[8,720,48]{1,2,0:T(8,128)} %get-tuple-element.262) | copy-start | bytes 3317764 | tf_op jit(solution)/shard_map/while
  225.0 9.2 %copy-start.6 = (f32[8,720]{1,0:T(8,128)S(1)}, f32[8,720]{1,0:T(8,128)}, u32[]{:S(2)}) copy-start(f32[8,720]{1,0:T(8,128)} %select_maximum_fusion.2) | copy-start | bytes 69124 | tf_op jit(solution)/shard_map/while
  246.9 11.2 %copy-start.3 = (f32[8,720,48]{1,2,0:T(8,128)S(1)}, f32[8,720,48]{1,2,0:T(8,128)}, u32[]{:S(2)}) copy-start(f32[8,720,48]{1,2,0:T(8,128)} %get-tuple-element.262) | copy-start | bytes 3317764 | tf_op jit(solution)/shard_map/while
  258.1 9.2 %copy-start.6 = (f32[8,720]{1,0:T(8,128)S(1)}, f32[8,720]{1,0:T(8,128)}, u32[]{:S(2)}) copy-start(f32[8,720]{1,0:T(8,128)} %select_maximum_fusion.2) | copy-start | bytes 69124 | tf_op jit(solution)/shard_map/while
  280.0 11.2 %copy-start.3 = (f32[8,720,48]{1,2,0:T(8,128)S(1)}, f32[8,720,48]{1,2,0:T(8,128)}, u32[]{:S(2)}) copy-start(f32[8,720,48]{1,2,0:T(8,128)} %get-tuple-element.262) | copy-start | bytes 3317764 | tf_op jit(solution)/shard_map/while
  291.2 9.2 %copy-start.6 = (f32[8,720]{1,0:T(8,128)S(1)}, f32[8,720]{1,0:T(8,128)}, u32[]{:S(2)}) copy-start(f32[8,720]{1,0:T(8,128)} %select_maximum_fusion.2) | copy-start | bytes 69124 | tf_op jit(solution)/shard_map/while
  313.1 11.2 %copy-start.3 = (f32[8,720,48]{1,2,0:T(8,128)S(1)}, f32[8,720,48]{1,2,0:T(8,128)}, u32[]{:S(2)}) copy-start(f32[8,720,48]{1,2,0:T(8,128)} %get-tuple-element.262) | copy-start | bytes 3317764 | tf_op jit(solution)/shard_map/while
  324.3 9.2 %copy-start.6 = (f32[8,720]{1,0:T(8,128)S(1)}, f32[8,720]{1,0:T(8,128)}, u32[]{:S(2)}) copy-start(f32[8,720]{1,0:T(8,128)} %select_maximum_fusion.2) | copy-start | bytes 69124 | tf_op jit(solution)/shard_map/while
  346.2 11.2 %copy-start.3 = (f32[8,720,48]{1,2,0:T(8,128)S(1)}, f32[8,720,48]{1,2,0:T(8,128)}, u32[]{:S(2)}) copy-start(f32[8,720,48]{1,2,0:T(8,128)} %get-tuple-element.262) | copy-start | bytes 3317764 | tf_op jit(solution)/shard_map/while
  357.4 9.2 %copy-start.6 = (f32[8,720]{1,0:T(8,128)S(1)}, f32[8,720]{1,0:T(8,128)}, u32[]{:S(2)}) copy-start(f32[8,720]{1,0:T(8,128)} %select_maximum_fusion.2) | copy-start | bytes 69124 | tf_op jit(solution)/shard_map/while
  369.0 93.0 %copy-start.2 = (bf16[720,1536]{1,0:T(8,128)(2,1)S(1)}, bf16[720,1536]{1,0:T(8,128)(2,1)}, u32[]{:S(2)}) copy-start(bf16[720,1536]{1,0:T(8,128)(2,1)} %param.9) | copy-start | bytes 6635524
  371.7 93.7 %copy-start.8 = (f32[1536]{0:T(1024)S(1)}, f32[1536]{0:T(1024)}, u32[]{:S(2)}) copy-start(f32[1536]{0:T(1024)} %param.13) | copy-start | bytes 18436
  371.7 196.0 %all-reduce.5.cloned.1.call-start = ((), (), s32[]{:S(2)}) async-start(), calls=%async_computation.3 | async-start | bytes 4423680 | tf_op jit(solution)/shard_map/psum | solution.py:77
  (10 other events, 19.2 us)
Sparse Core Ops, SparseCore 0:
  23.7 40.2 all-gather.4
  65.9 37.5 all-gather.2
  371.8 90.1 all-reduce.2
  478.5 89.1 all-reduce.4
where the time goes:
time: 580 us; the launch traced here: 579 us
  waiting for transfers between devices  259 us (45%)
  matrix products  163 us (28%)
  other arithmetic  113 us (19%)
  local copies, waits for them, and re-layouts  30.3 us (5%)
  between operations  13.2 us (2%)
    psum x1, waiting for transfers between devices, per_device(): lax.psum(attn_term.astype(jnp.bfloat16), 'tensor').astype(jnp.float32)  90 us
    psum x1, waiting for transfers between devices, per_device(): lax.psum(mlp_term.astype(jnp.bfloat16), 'tensor').astype(jnp.float32)  89.3 us
    reduce_sum x8, other arithmetic, attend_block(): total = total * factor + jnp.sum(weights, axis=-1)  77.9 us
    dot_general x8, matrix products, attend_block(): jnp.einsum('hqk,khd->hqd', weights.astype(jnp.bfloat16), values, preferre...  73.3 us
    dot_general x8, matrix products, attend_block(): jnp.einsum('qhd,khd->hqk', queries, keys, preferred_element_type=jnp.floa...  68.5 us
    all_gather x1, waiting for transfers between devices, per_device(): key_piece = lax.all_gather(key, 'seq', axis=0, tiled=True)  39.5 us
    all_gather x1, waiting for transfers between devices, per_device(): value_piece = lax.all_gather(value, 'seq', axis=0, tiled=True)  39.2 us
    dot_general x1, matrix products, per_device(): mlp_term = jnp.dot(hidden, w_down, preferred_element_type=jnp.float32)  12.9 us
  transfers between devices with their start and end apart: 4, of which 4 were waited for; matrix products, arithmetic and copies ran while one was open for 0% of the time, Pallas kernels for 0%

commit v1 on v0

v1 whole, which is shorter than its diff:
```python
import functools

import jax
import jax.numpy as jnp
from jax import lax
from jax.experimental import pallas as pl
from jax.experimental.pallas import tpu as pltpu
from jax.sharding import PartitionSpec as P

HD = 48
ONES = 16
LOG2E = 1.4426950408889634
MESH = pl.DeviceIdType.MESH
CONTRACT_FIRST = (((0,), (0,)), ((), ()))


def layer_norm(values, gain):
    mean = jnp.mean(values, axis=-1, keepdims=True)
    centred = values - mean
    var = jnp.mean(centred * centred, axis=-1, keepdims=True)
    return centred * lax.rsqrt(var + 1e-05) * gain


def flip(chip, mask, chips):
    result, bit = 0, 1
    while bit < chips:
        mine, other = (chip // bit) % 2, (mask // bit) % 2
        result = result + bit * (mine + other - 2 * mine * other)
        bit *= 2
    return result


def attend_kernel(n, heads, group, q_ref, kv_ref, o_ref, held, accum, peak, own_sem, send_sem, pass_sem, recv_sem):
    seq, lane = lax.axis_index("seq"), lax.axis_index("tensor")
    chips = n // 2
    chip, core = seq // 2, seq % 2
    sibling = chip * 2 + 1 - core

    def order(step, which):
        if chips < 4:
            return step + 1
        return step + 1 + which * (jnp.where(step == 0, 1, 0) - jnp.where(step == 1, 1, 0))

    def send(source, slot, target, sem):
        return pltpu.make_async_remote_copy(
            src_ref=source,
            dst_ref=held.at[slot],
            send_sem=sem,
            recv_sem=recv_sem.at[slot],
            device_id=(target, lane),
            device_id_type=MESH,
        )

    barrier = pltpu.get_barrier_semaphore()
    pl.semaphore_signal(barrier, inc=1, device_id=(sibling, lane), device_id_type=MESH)
    for step in range(1, chips):
        pl.semaphore_signal(
            barrier, inc=1, device_id=(flip(chip, step, chips) * 2 + core, lane), device_id_type=MESH
        )
    pl.semaphore_wait(barrier, chips)

    for step in range(chips - 1):
        target = flip(chip, order(step, core), chips) * 2 + core
        send(kv_ref, seq, target, send_sem.at[step]).start()
    send(kv_ref, seq, sibling, pass_sem.at[chips - 1]).start()
    own = pltpu.make_async_copy(kv_ref, held.at[seq], own_sem)
    own.start()
    accum[...] = jnp.zeros_like(accum)
    peak[...] = jnp.full_like(peak, -1e30)
    own.wait()

    def attend(slot):
        @pl.loop(0, heads // group)
        def _(index):
            members = [index * group + offset for offset in range(group)]
            scores = [
                lax.dot_general(held[slot, h], q_ref[h], CONTRACT_FIRST, preferred_element_type=jnp.float32)
                for h in members
            ]
            for h, score in zip(members, scores):
                value = held[slot, heads + h]
                value = jnp.concatenate([value, jnp.ones((ONES, value.shape[1]), value.dtype)], axis=0)
                old = peak[h]
                new = jnp.maximum(old, jnp.max(score, axis=0, keepdims=True))
                weights = jnp.exp2(score - new).astype(jnp.bfloat16)
                term = jnp.dot(value, weights, preferred_element_type=jnp.float32)
                accum[h] = accum[h] * jnp.exp2(old - new) + term
                peak[h] = new

    @pl.loop(0, n)
    def _(index):
        step, second = index // 2, index % 2
        which = core + second - 2 * core * second
        mask = jnp.where(step == 0, 0, order(step - 1, which))
        slot = flip(chip, mask, chips) * 2 + which

        @pl.when(index > 0)
        def _():
            send(held.at[slot], slot, sibling, pass_sem.at[0]).wait_recv()

        @pl.when(jnp.logical_and(index > 0, second == 0))
        def _():
            send(held.at[slot], slot, sibling, pass_sem.at[step - 1]).start()

        attend(slot)

    for h in range(heads):
        o_ref[h] = (accum[h, :HD] / accum[h, HD : HD + 1]).astype(o_ref.dtype)

    for step in range(chips - 1):
        send(kv_ref, seq, sibling, send_sem.at[step]).wait_send()
    for step in range(chips):
        send(kv_ref, seq, sibling, pass_sem.at[step]).wait_send()


def attention(n, heads, query, pairs):
    rows = query.shape[2]
    group = next(size for size in (4, 2, 1) if heads % size == 0)
    vmem = pl.BlockSpec(memory_space=pltpu.VMEM)
    return pl.pallas_call(
        functools.partial(attend_kernel, n, heads, group),
        out_shape=jax.ShapeDtypeStruct((heads, HD, rows), jnp.bfloat16),
        in_specs=[vmem, vmem],
        out_specs=vmem,
        scratch_shapes=[
            pltpu.VMEM((n, 2 * heads, HD, rows), jnp.bfloat16),
            pltpu.VMEM((heads, HD + ONES, rows), jnp.float32),
            pltpu.VMEM((heads, 1, rows), jnp.float32),
            pltpu.SemaphoreType.DMA,
            pltpu.SemaphoreType.DMA((n // 2,)),
            pltpu.SemaphoreType.DMA((n // 2,)),
            pltpu.SemaphoreType.DMA((n,)),
        ],
        compiler_params=pltpu.CompilerParams(
            collective_id=0, has_side_effects=True, vmem_limit_bytes=56 * 2**20
        ),
    )(query, pairs)


def per_device(n, tokens, norm_gain, w_qkv, w_out, post_gain, w_up, w_down):
    rows = tokens.shape[0]
    span = w_qkv.shape[2]
    heads = span // HD
    base = tokens.astype(jnp.float32)
    normed = layer_norm(base, norm_gain).astype(jnp.bfloat16)
    weights = w_qkv.reshape(w_qkv.shape[0], -1)
    qkv = lax.dot_general(weights, normed, (((0,), (1,)), ((), ())), preferred_element_type=jnp.float32)
    query = (qkv[:span] * (LOG2E / HD**0.5)).astype(jnp.bfloat16).reshape(heads, HD, rows)
    pairs = qkv[span:].astype(jnp.bfloat16).reshape(2 * heads, HD, rows)
    attended = attention(n, heads, query, pairs).reshape(span, rows)
    attn_term = lax.dot_general(attended, w_out, CONTRACT_FIRST, preferred_element_type=jnp.float32)
    mixed = base + lax.psum(attn_term.astype(jnp.bfloat16), "tensor").astype(jnp.float32)
    post = layer_norm(mixed, post_gain).astype(jnp.bfloat16)
    hidden = jax.nn.gelu(
        jnp.dot(post, w_up, preferred_element_type=jnp.float32), approximate=True
    ).astype(jnp.bfloat16)
    mlp_term = jnp.dot(hidden, w_down, preferred_element_type=jnp.float32)
    return (mixed + lax.psum(mlp_term.astype(jnp.bfloat16), "tensor").astype(jnp.float32)).astype(
        jnp.bfloat16
    )


def solution(mesh):
    placed = (
        P("seq", None),
        P(),
        P(None, None, "tensor"),
        P("tensor", None),
        P(),
        P(None, "tensor"),
        P("tensor", None),
    )
    return jax.shard_map(
        functools.partial(per_device, mesh.shape["seq"]),
        mesh=mesh,
        in_specs=placed,
        out_specs=P("seq", None),
        check_vma=False,
    )
```

time: 580 us -> 311 us (0.54)
  matrix products: 163 us -> 21.8 us
  other arithmetic: 113 us -> 13.4 us
  waiting for transfers between devices: 259 us -> 180 us
  Pallas kernels: 0 us -> 69.9 us
  local copies, waits for them, and re-layouts: 30.3 us -> 11.7 us
    dot_general x18 -> x2, matrix products: 150 us -> 8.9 us  [the longest x1 5.14 us: per_device(): lax.dot_general(weights, normed, (((0,), (1,)), ((), ())), preferred_elem...]
    all_gather x2 -> x0, waiting for transfers between devices: 78.6 us -> none  [the longest x1 39.5 us: per_device(): key_piece = lax.all_gather(key, 'seq', axis=0, tiled=True)]
    reduce_sum x8 -> x0, other arithmetic: 77.9 us -> none  [attend_block(): total = total * factor + jnp.sum(weights, axis=-1)]
    pallas_call x0 -> x1, Pallas kernels: none -> 69.9 us  [attention(): pl.pallas_call(functools.partial(attend_kernel, n, heads, group), out_sha...]
    dynamic_slice x24 -> x0, local copies, waits for them, and re-layouts: 14.7 us -> none  [the longest x16 12.6 us: step(): value_block = lax.dynamic_slice_in_dim(value_piece, first, block, 0)]
    add x8 -> x0, other arithmetic: 11.4 us -> none  [attend_block(): total = total * factor + jnp.sum(weights, axis=-1)]
    max x8 -> x0, other arithmetic: 9.98 us -> none  [attend_block(): fresh = jnp.maximum(peak, jnp.max(scores, axis=-1))]
    while x56 -> x0, local copies, waits for them, and re-layouts: 8.1 us -> none
  transfers between devices with their start and end apart: 4 -> 2, of which waited for: 4 -> 2; matrix products, arithmetic and copies ran while one was open for 0% -> 0% of each run, Pallas kernels for 0% -> 0%
where the time goes in v1:
time: 311 us
  waiting for transfers between devices  180 us (58%)
  Pallas kernels  69.9 us (22%)
  matrix products  21.8 us (7%)
  between operations  13.5 us (4%)
  other arithmetic  13.4 us (4%)
  local copies, waits for them, and re-layouts  11.7 us (4%)
    psum x1, waiting for transfers between devices, per_device(): lax.psum(attn_term.astype(jnp.bfloat16), 'tensor').astype(jnp.float32)  90.8 us
    psum x1, waiting for transfers between devices, per_device(): lax.psum(mlp_term.astype(jnp.bfloat16), 'tensor').astype(jnp.float32)  89.3 us
    pallas_call x1, Pallas kernels, attention(): pl.pallas_call(functools.partial(attend_kernel, n, heads, group), out_sha...  69.9 us
    dot_general x1, matrix products, per_device(): mlp_term = jnp.dot(hidden, w_down, preferred_element_type=jnp.float32)  12.9 us
  transfers between devices with their start and end apart: 2, of which 2 were waited for; matrix products, arithmetic and copies ran while one was open for 0% of the time, Pallas kernels for 0%

profile of v1, /device:TPU:0, one launch (start us, length us, event | category | flops | bytes accessed | tf_op | source)
XLA Modules:
  0.0 310.7 jit_solution(2986438523619918318)
XLA Ops:
  6.5 0.0 copy-start
  6.5 2.1 convert_reduce_fusion
  8.6 0.0 copy-start.1
  8.6 0.0 copy-start.3
  8.7 2.5 fusion.2
  11.1 6.1 %copy.10 = bf16[1536,3,384]{0,2,1:T(8,128)(2,1)} copy(bf16[1536,3,384]{2,0,1:T(8,128)(2,1)} %param.9) | data formatting | bytes 7077888 | tf_op args[2]
  17.2 5.1 %convolution_bitcast_fusion = f32[1152,720]{0,1:T(8,128)S(1)} fusion(bf16[1536,1152]{0,1:T(8,128)(2,1)} %bitcast.12, bf16[720,1536]{1,0:T(8,128)(2,1)S(1)} %copy-done.1, f32[1536]{0:T(1024)S(1)} %copy-done.3, f32[720]{0:T(1024)S(1)} %add_rsqrt_fusion.1, f32[720]{0:T(1024)S(1)} %broadcast_multiply_fusion.1), kind=kOutput, calls=%fused_computation.20 | convolution fusion | flops 2553569280 | bytes 9080448 | tf_op jit(solution)/shard_map/dot_general | solution.py:147
  22.4 0.9 fusion.22
  23.3 1.1 slice.15
  24.4 2.1 copy.11
  26.5 2.4 copy.12
  28.9 69.9 %shard_map.73 = bf16[8,48,720]{2,1,0:T(8,128)(2,1)} custom-call(bf16[8,48,720]{2,1,0:T(8,128)(2,1)} %bitcast.13, bf16[16,48,720]{2,1,0:T(8,128)(2,1)} %bitcast.11), custom_call_target="tpu_custom_call" | custom-call | tf_op jit(solution)/shard_map/pallas_call | solution.py:120
  98.8 3.8 %convolution_convert_fusion.1 = bf16[720,1536]{1,0:T(8,128)(2,1)} fusion(bf16[384,720]{1,0:T(8,128)(2,1)} %bitcast.14, bf16[384,1536]{1,0:T(8,128)(2,1)S(1)} %copy-done), kind=kOutput, calls=%fused_computation.23 | convolution fusion | flops 850452480 | bytes 3944448 | tf_op jit(solution)/shard_map/dot_general | solution.py:151
  102.5 0.0 all-reduce.3.cloned.1.call-update
  102.6 0.0 copy-start.4
  102.6 0.2 all-reduce.5.cloned.1.call-start
  102.8 90.8 %all-reduce.3.cloned.1.call-done = bf16[720,1536]{1,0:T(8,128)(2,1)} async-done(((bf16[720,1536]{1,0:T(8,128)(2,1)}), bf16[720,1536]{1,0:T(8,128)(2,1)}) %all-reduce.3.cloned.1.call-update) | async-done | bytes 2211856 | tf_op jit(solution)/shard_map/psum | solution.py:152
  193.6 2.4 fusion.13
  196.1 1.0 multiply_reduce_fusion
  197.1 0.0 copy-done.4
  197.1 12.9 %convolution_convert_fusion = bf16[720,1536]{1,0:T(8,128)(2,1)} fusion(bf16[1536,1536]{1,0:T(8,128)(2,1)} %param.13, bf16[1536,1536]{1,0:T(8,128)(2,1)} %param.12, bf16[720,1536]{1,0:T(8,128)(2,1)} %all-reduce.3.cloned.1.call-done, bf16[720,1536]{1,0:T(8,128)(2,1)S(1)} %copy-done.1, f32[1536]{0:T(1024)S(1)} %copy-done.4, f32[720]{0:T(1024)S(1)} %add_rsqrt_fusion, ...), kind=kOutput, calls=%fused_computation.22 | convolution fusion | flops 6813573120 | bytes 16084608 | tf_op jit(solution)/shard_map/dot_general | solution.py:157
  210.0 0.0 all-reduce.5.cloned.1.call-update
  210.0 89.3 %all-reduce.5.cloned.1.call-done = bf16[720,1536]{1,0:T(8,128)(2,1)} async-done(((bf16[720,1536]{1,0:T(8,128)(2,1)}), bf16[720,1536]{1,0:T(8,128)(2,1)}) %all-reduce.5.cloned.1.call-update) | async-done | bytes 2211856 | tf_op jit(solution)/shard_map/psum | solution.py:158
  299.3 4.5 %add_convert_fusion = bf16[720,1536]{1,0:T(8,128)(2,1)} fusion(bf16[720,1536]{1,0:T(8,128)(2,1)} %all-reduce.5.cloned.1.call-done, bf16[720,1536]{1,0:T(8,128)(2,1)} %all-reduce.3.cloned.1.call-done, bf16[720,1536]{1,0:T(8,128)(2,1)S(1)} %copy-done.1), kind=kLoop, calls=%fused_computation.17 | loop fusion | flops 6635520 | bytes 8847360 | tf_op jit(solution)/shard_map/convert_element_type | solution.py:158
  (10 shorter events, 0.0 us)
Async XLA Ops:
  6.5 92.2 %copy-start = (bf16[384,1536]{1,0:T(8,128)(2,1)S(1)}, bf16[384,1536]{1,0:T(8,128)(2,1)}, u32[]{:S(2)}) copy-start(bf16[384,1536]{1,0:T(8,128)(2,1)} %param.10) | copy-start | bytes 3538948
  6.5 187.1 %all-reduce.3.cloned.1.call-start = ((), (), s32[]{:S(2)}) async-start(), calls=%async_computation | async-start | bytes 4423680 | tf_op jit(solution)/shard_map/psum | solution.py:152
  8.6 8.6 %copy-start.1 = (bf16[720,1536]{1,0:T(8,128)(2,1)S(1)}, bf16[720,1536]{1,0:T(8,128)(2,1)}, u32[]{:S(2)}) copy-start(bf16[720,1536]{1,0:T(8,128)(2,1)} %param.7) | copy-start | bytes 6635524
  8.6 8.6 %copy-start.3 = (f32[1536]{0:T(1024)S(1)}, f32[1536]{0:T(1024)}, u32[]{:S(2)}) copy-start(f32[1536]{0:T(1024)} %param.8) | copy-start | bytes 18436
  102.6 94.5 %copy-start.4 = (f32[1536]{0:T(1024)S(1)}, f32[1536]{0:T(1024)}, u32[]{:S(2)}) copy-start(f32[1536]{0:T(1024)} %param.11) | copy-start | bytes 18436
  102.6 196.7 %all-reduce.5.cloned.1.call-start = ((), (), s32[]{:S(2)}) async-start(), calls=%async_computation.1 | async-start | bytes 4423680 | tf_op jit(solution)/shard_map/psum | solution.py:158
  193.6 2.4 copy-start.2
Sparse Core Ops, SparseCore 0:
  102.7 90.8 all-reduce.2
  210.1 89.1 all-reduce.4

commit v2 on v1

--- a/solution.py
+++ b/solution.py
@@ -6,6 +6,7 @@
 from jax.experimental import pallas as pl
 from jax.experimental.pallas import tpu as pltpu
 from jax.sharding import PartitionSpec as P
+
 
 HD = 48
 ONES = 16
@@ -134,6 +135,11 @@
         compiler_params=pltpu.CompilerParams(
             collective_id=0, has_side_effects=True, vmem_limit_bytes=56 * 2**20
         ),
+        cost_estimate=pl.CostEstimate(
+            flops=4 * n * heads * rows * rows * HD,
+            bytes_accessed=6 * heads * HD * rows,
+            transcendentals=n * heads * rows * rows,
+        ),
     )(query, pairs)
 
 
@@ -147,9 +153,11 @@
     qkv = lax.dot_general(weights, normed, (((0,), (1,)), ((), ())), preferred_element_type=jnp.float32)
     query = (qkv[:span] * (LOG2E / HD**0.5)).astype(jnp.bfloat16).reshape(heads, HD, rows)
     pairs = qkv[span:].astype(jnp.bfloat16).reshape(2 * heads, HD, rows)
-    attended = attention(n, heads, query, pairs).reshape(span, rows)
-    attn_term = lax.dot_general(attended, w_out, CONTRACT_FIRST, preferred_element_type=jnp.float32)
-    mixed = base + lax.psum(attn_term.astype(jnp.bfloat16), "tensor").astype(jnp.float32)
+    w_full = lax.all_gather(w_out, "tensor", axis=0, tiled=True)
+    attended = attention(n, heads, query, pairs)
+    attended = attended.reshape(span, rows)
+    attended = lax.all_gather(attended, "tensor", axis=0, tiled=True)
+    mixed = base + lax.dot_general(attended, w_full, CONTRACT_FIRST, preferred_element_type=jnp.float32)
     post = layer_norm(mixed, post_gain).astype(jnp.bfloat16)
     hidden = jax.nn.gelu(
         jnp.dot(post, w_up, preferred_element_type=jnp.float32), approximate=True

time: 311 us -> 361 us (1.16)
  waiting for transfers between devices: 180 us -> 229 us
    all_gather x0 -> x2, waiting for transfers between devices: none -> 140 us  [the longest x1 89.7 us: per_device(): w_full = lax.all_gather(w_out, 'tensor', axis=0, tiled=True)]
    psum x1 -> x0, waiting for transfers between devices: 90.8 us -> none  [per_device(): lax.psum(attn_term.astype(jnp.bfloat16), 'tensor').astype(jnp.float32)]
    unnamed x11 -> x9, local copies, waits for them, and re-layouts: 6.11 us -> 8.08 us
  transfers between devices with their start and end apart: 2 -> 3, of which waited for: 2 -> 3; matrix products, arithmetic and copies ran while one was open for 0% -> 0% of each run, Pallas kernels for 0% -> 0%
where the time goes in v2:
time: 361 us; the launch traced here: 360 us
  waiting for transfers between devices  229 us (63%)
  Pallas kernels  69.9 us (19%)
  matrix products  25.3 us (7%)
  between operations  13.2 us (4%)
  local copies, waits for them, and re-layouts  11.7 us (3%)
  other arithmetic  11 us (3%)
    all_gather x1, waiting for transfers between devices, per_device(): w_full = lax.all_gather(w_out, 'tensor', axis=0, tiled=True)  89.7 us
    psum x1, waiting for transfers between devices, per_device(): lax.psum(mlp_term.astype(jnp.bfloat16), 'tensor').astype(jnp.float32)  88.7 us
    pallas_call x1, Pallas kernels, attention(): pl.pallas_call(functools.partial(attend_kernel, n, heads, group), out_sha...  69.9 us
    all_gather x1, waiting for transfers between devices, per_device(): attended = lax.all_gather(attended, 'tensor', axis=0, tiled=True)  49.9 us
    dot_general x1, matrix products, per_device(): mlp_term = jnp.dot(hidden, w_down, preferred_element_type=jnp.float32)  13.5 us
    unnamed x9, local copies, waits for them, and re-layouts  8.08 us
  transfers between devices with their start and end apart: 3, of which 3 were waited for; matrix products, arithmetic and copies ran while one was open for 0% of the time, Pallas kernels for 0%

profile of v2, /device:TPU:0, one launch (start us, length us, event | category | flops | bytes accessed | tf_op | source)
XLA Modules:
  0.0 360.5 jit_solution(2780538651284638869)
XLA Ops:
  6.5 2.0 convert_reduce_fusion
  8.5 0.0 copy-start.1
  8.5 0.0 copy-start.2
  8.6 2.5 fusion.2
  11.1 6.1 %copy.10 = bf16[1536,3,384]{0,2,1:T(8,128)(2,1)} copy(bf16[1536,3,384]{2,0,1:T(8,128)(2,1)} %param.9) | data formatting | bytes 7077888 | tf_op args[2]
  17.1 5.1 %convolution_bitcast_fusion = f32[1152,720]{0,1:T(8,128)S(1)} fusion(bf16[1536,1152]{0,1:T(8,128)(2,1)} %bitcast.11, bf16[720,1536]{1,0:T(8,128)(2,1)S(1)} %copy-done.1, f32[1536]{0:T(1024)S(1)} %copy-done.2, f32[720]{0:T(1024)S(1)} %add_rsqrt_fusion.1, f32[720]{0:T(1024)S(1)} %broadcast_multiply_fusion.1), kind=kOutput, calls=%fused_computation.20 | convolution fusion | flops 2553569280 | bytes 9080448 | tf_op jit(solution)/shard_map/dot_general | solution.py:153
  22.3 0.1 slice.15
  22.4 0.9 fusion.21
  23.3 1.4 copy.12
  24.8 2.1 copy.11
  26.8 69.9 %shard_map.73 = bf16[8,48,720]{2,1,0:T(8,128)(2,1)} custom-call(bf16[8,48,720]{2,1,0:T(8,128)(2,1)} %bitcast.14, bf16[16,48,720]{2,1,0:T(8,128)(2,1)} %bitcast.12), custom_call_target="tpu_custom_call" | custom-call | flops 6370099200 | bytes 1658880 | tf_op jit(solution)/shard_map/pallas_call | solution.py:121
  96.7 0.0 all-gather.3.cloned.1.call-update
  96.8 0.0 all-gather.5.cloned.1.call-start
  96.8 0.7 all-gather.5.cloned.1.call-update
  97.5 0.2 all-reduce.2.cloned.1.call-start
  97.8 49.9 %all-gather.3.cloned.1.call-done = bf16[1536,720]{1,0:T(8,128)(2,1)} async-done(((bf16[384,720]{1,0:T(8,128)(2,1)}), bf16[1536,720]{1,0:T(8,128)(2,1)}) %all-gather.3.cloned.1.call-update) | async-done | bytes 2211856 | tf_op jit(solution)/shard_map/all_gather | solution.py:159
  147.7 89.7 %all-gather.5.cloned.1.call-done = bf16[1536,1536]{1,0:T(8,128)(2,1)} async-done(((bf16[384,1536]{1,0:T(8,128)(2,1)}), bf16[1536,1536]{1,0:T(8,128)(2,1)}) %all-gather.5.cloned.1.call-update) | async-done | bytes 4718608 | tf_op jit(solution)/shard_map/all_gather | solution.py:156
  237.4 6.6 %fusion.26 = (f32[720]{0:T(1024)S(1)}, f32[720,1536]{1,0:T(8,128)S(1)}) fusion(bf16[1536,720]{1,0:T(8,128)(2,1)} %all-gather.3.cloned.1.call-done, bf16[1536,1536]{1,0:T(8,128)(2,1)} %all-gather.5.cloned.1.call-done, bf16[720,1536]{1,0:T(8,128)(2,1)S(1)} %copy-done.1), kind=kOutput, calls=%fused_computation.40 | convolution fusion | flops 3400703232 | bytes 13568832 | tf_op jit(solution)/shard_map/dot_general | solution.py:160
  244.0 2.0 copy-done
  246.0 0.6 multiply_reduce_fusion
  246.6 13.5 %convolution_convert_fusion = bf16[720,1536]{1,0:T(8,128)(2,1)} fusion(bf16[1536,1536]{1,0:T(8,128)(2,1)} %param.13, bf16[1536,1536]{1,0:T(8,128)(2,1)} %param.12, f32[720,1536]{1,0:T(8,128)} %copy-done, f32[1536]{0:T(1024)S(1)} %copy-done.3, f32[720]{0:T(1024)S(1)} %add_rsqrt_fusion, f32[720]{0:T(1024)S(1)} %broadcast_multiply_fusion), kind=kOutput, calls=%fused_computation.21 | convolution fusion | flops 6810255360 | bytes 16084608 | tf_op jit(solution)/shard_map/dot_general | solution.py:165
  260.2 0.0 all-reduce.2.cloned.1.call-update
  260.2 88.7 %all-reduce.2.cloned.1.call-done = bf16[720,1536]{1,0:T(8,128)(2,1)} async-done(((bf16[720,1536]{1,0:T(8,128)(2,1)}), bf16[720,1536]{1,0:T(8,128)(2,1)}) %all-reduce.2.cloned.1.call-update) | async-done | bytes 2211856 | tf_op jit(solution)/shard_map/psum | solution.py:166
  348.9 5.0 %add_convert_fusion = bf16[720,1536]{1,0:T(8,128)(2,1)} fusion(f32[720,1536]{1,0:T(8,128)} %copy-done, bf16[720,1536]{1,0:T(8,128)(2,1)} %all-reduce.2.cloned.1.call-done), kind=kLoop, calls=%fused_computation.17 | loop fusion | flops 3317760 | bytes 8847360 | tf_op jit(solution)/shard_map/convert_element_type | solution.py:166
  (10 shorter events, 0.0 us)
Async XLA Ops:
  6.5 141.2 %all-gather.3.cloned.1.call-start = ((), (), s32[]{:S(2)}) async-start(), calls=%async_computation | async-start | bytes 2949120 | tf_op jit(solution)/shard_map/all_gather | solution.py:159
  8.5 8.6 %copy-start.1 = (bf16[720,1536]{1,0:T(8,128)(2,1)S(1)}, bf16[720,1536]{1,0:T(8,128)(2,1)}, u32[]{:S(2)}) copy-start(bf16[720,1536]{1,0:T(8,128)(2,1)} %param.7) | copy-start | bytes 6635524
  8.5 8.6 %copy-start.2 = (f32[1536]{0:T(1024)S(1)}, f32[1536]{0:T(1024)}, u32[]{:S(2)}) copy-start(f32[1536]{0:T(1024)} %param.8) | copy-start | bytes 18436
  96.8 140.7 %all-gather.5.cloned.1.call-start = ((), (), s32[]{:S(2)}) async-start(), calls=%async_computation.1 | async-start | bytes 5898240 | tf_op jit(solution)/shard_map/all_gather | solution.py:156
  97.5 251.4 %all-reduce.2.cloned.1.call-start = ((), (), s32[]{:S(2)}) async-start(), calls=%async_computation.2 | async-start | bytes 4423680 | tf_op jit(solution)/shard_map/psum | solution.py:166
  244.0 2.0 copy-start
  244.0 2.6 copy-start.3
Sparse Core Ops, SparseCore 0:
  96.9 50.7 all-gather.2
  149.3 88.1 all-gather.4
  260.3 88.5 all-reduce.1
